TPU v7x, 32 devices: a whole 2x2x4 slice. The times are simulated.
32 devices in a mesh: layer: 2 (over x), row: 4 (over z), col: 4 (over y, core).
Axes of the slice: x: 2, y: 2, z: 4, core: 2. Of those that a mesh axis runs over, the one named last changes fastest.
Arguments:
- left_matrix: float32 [2, 1024, 16384], P(None, 'row', 'col'), may hold values from -6 to 6
- right_matrix: float32 [2, 16384, 512], P(None, 'row', 'col'), may hold values from -0.03125 to 0.03125
Outputs:
- product: float32 [2, 1024, 512], P(None, 'row', 'col')
All inputs are finite; a program needn't handle non-finite values.
Results may differ from a plain program's by a relative error of at most 0.000071.
Values sent between devices are 32-bit elements; how exact they have to be, the bound alone decides.
A program may use at most 128 MiB of HBM per device.

v0:
```python
import jax
import jax.numpy as jnp
from jax import lax
from jax.sharding import PartitionSpec as P


def gauss_fold(right_whole, site_rows, cols_out):
    right_real = right_whole[0]
    right_imag = right_whole[1]
    right_total = right_real + right_imag
    highest = lax.Precision.HIGHEST
    empty = jnp.zeros((site_rows, cols_out), jnp.float32)

    def accumulate(totals, segment, offset):
        left_real = segment[0]
        left_imag = segment[1]
        first_term = jnp.dot(
            left_real, right_real, precision=highest, preferred_element_type=jnp.float32
        )
        second_term = jnp.dot(
            left_imag, right_imag, precision=highest, preferred_element_type=jnp.float32
        )
        third_term = jnp.dot(
            left_real + left_imag,
            right_total,
            precision=highest,
            preferred_element_type=jnp.float32,
        )
        return (first_term, second_term, third_term)

    return (accumulate, (empty, empty, empty))


def combine_terms(totals):
    first_term, second_term, third_term = totals
    return jnp.stack([first_term - second_term, third_term - first_term - second_term])


def local(left_matrix, right_matrix):
    layers = lax.axis_size("layer")
    layer_index = lax.axis_index("layer")
    local_rows = left_matrix.shape[1]
    local_cols = right_matrix.shape[2]
    left_width = left_matrix.shape[2]
    right_height = right_matrix.shape[1]
    share_width = left_width // layers
    group_count = right_height // left_width
    left_own = lax.dynamic_slice_in_dim(left_matrix, layer_index * share_width, share_width, 2)
    right_view = right_matrix.reshape(2, group_count, layers, share_width, local_cols)
    right_own = lax.dynamic_slice_in_dim(right_view, layer_index, 1, 2)
    right_own = right_own.reshape(2, group_count * share_width, local_cols)
    right_whole = lax.all_gather(right_own, "row", axis=1, tiled=True)
    accumulate, initial = gauss_fold(right_whole, local_rows, local_cols)
    totals = accumulate(initial, lax.all_gather(left_own, "col", axis=2, tiled=True), jnp.int32(0))
    partial_product = combine_terms(totals)
    product = lax.psum(partial_product, "layer")
    return product


def solution(mesh):
    in_specs = (P(None, "row", "col"), P(None, "row", "col"))
    out_specs = P(None, "row", "col")
    return jax.shard_map(local, mesh=mesh, in_specs=in_specs, out_specs=out_specs, check_vma=False)
```

profile of v0, /device:TPU:0, one launch (start us, length us, event | category | flops | bytes accessed | tf_op | source)
XLA Modules:
  0.0 329.2 jit_solution(11281705026312441378)
XLA Ops:
  6.5 0.0 all-gather.6.cloned.1.call-start
  6.5 3.1 constant_dynamic-slice_fusion
  9.6 0.0 all-gather.6.cloned.1.call-update
  9.6 0.0 all-gather.4.cloned.1.call-start
  9.7 4.7 %constant_dynamic-slice_fusion.1 = f32[2,256,2048]{2,1,0:T(8,128)} fusion(f32[2,256,4096]{2,1,0:T(8,128)} %param.2, s32[]{:T(128)S(6)} %select_n.6), kind=kLoop, calls=%fused_computation.25 | loop fusion | bytes 8388612 | tf_op jit(solution)/shard_map/dynamic_slice | solution.py:48
  14.3 0.0 all-gather.4.cloned.1.call-update
  14.3 0.0 all-reduce.2.cloned.1.call-start
  14.4 147.7 %all-gather.6.cloned.1.call-done = f32[2,1,1,8192,128]{4,3,2,0,1:T(8,128)} async-done(((f32[2,1,1,2048,128]{4,3,2,0,1:T(8,128)}), f32[2,1,1,8192,128]{4,3,2,0,1:T(8,128)}) %all-gather.6.cloned.1.call-update) | async-done | bytes 8388624 | tf_op jit(solution)/shard_map/all_gather | solution.py:52
  162.1 105.7 %all-gather.4.cloned.1.call-done = f32[2,256,8192]{2,1,0:T(8,128)} async-done(((f32[2,256,2048]{2,1,0:T(8,128)}), f32[2,256,8192]{2,1,0:T(8,128)}) %all-gather.4.cloned.1.call-update) | async-done | bytes 16777232 | tf_op jit(solution)/shard_map/all_gather | solution.py:54
  267.8 0.0 copy-start
  267.8 9.9 %fusion.4 = f32[256,128]{1,0:T(8,128)S(1)} fusion(f32[2,256,8192]{2,1,0:T(8,128)} %all-gather.4.cloned.1.call-done, f32[2,1,1,8192,128]{4,3,2,0,1:T(8,128)} %all-gather.6.cloned.1.call-done), kind=kOutput, calls=%fused_computation.4 | convolution fusion | flops 3221225472 | bytes 12713984 | tf_op jit(solution)/shard_map/dot_general | solution.py:17
  277.7 9.8 %fusion.2 = f32[256,128]{1,0:T(8,128)S(1)} fusion(f32[2,256,8192]{2,1,0:T(8,128)} %all-gather.4.cloned.1.call-done, f32[2,1,1,8192,128]{4,3,2,0,1:T(8,128)} %all-gather.6.cloned.1.call-done), kind=kOutput, calls=%fused_computation.2 | convolution fusion | flops 3221225472 | bytes 12713984 | tf_op jit(solution)/shard_map/dot_general | solution.py:20
  287.6 0.0 copy-done
  287.6 9.2 %fusion.29 = f32[1,256,128]{2,1,0:T(8,128)S(1)} fusion(f32[256,128]{1,0:T(8,128)S(1)} %fusion.2, f32[256,128]{1,0:T(8,128)S(1)} %fusion.4, f32[2,1,1,8192,128]{4,3,2,0,1:T(8,128)} %all-gather.6.cloned.1.call-done, f32[2,256,8192]{2,1,0:T(8,128)S(1)} %copy-done), kind=kOutput, calls=%fused_computation.21 | convolution fusion | flops 3224436736 | bytes 25559040 | tf_op jit(solution)/shard_map/dot_general | solution.py:23
  296.8 0.7 pad_maximum_fusion
  297.5 0.0 all-reduce.2.cloned.1.call-update
  297.5 23.4 %all-reduce.2.cloned.1.call-done = f32[2,256,128]{2,1,0:T(8,128)} async-done(((f32[2,256,128]{2,1,0:T(8,128)}), f32[2,256,128]{2,1,0:T(8,128)}) %all-reduce.2.cloned.1.call-update) | async-done | bytes 262160 | tf_op jit(solution)/shard_map/psum | solution.py:56
  321.0 1.7 copy.4
  (1 shorter events, 0.0 us)
Async XLA Ops:
  6.5 155.6 %all-gather.6.cloned.1.call-start = ((), (), s32[]{:S(2)}) async-start(), calls=%async_computation.2 | async-start | bytes 10485760 | tf_op jit(solution)/shard_map/all_gather | solution.py:52
  9.6 258.2 %all-gather.4.cloned.1.call-start = ((), (), s32[]{:S(2)}) async-start(), calls=%async_computation | async-start | bytes 20971520 | tf_op jit(solution)/shard_map/all_gather | solution.py:54
  14.3 306.6 %all-reduce.2.cloned.1.call-start = ((), (), s32[]{:S(2)}) async-start(), calls=%async_computation.1 | async-start | bytes 524288 | tf_op jit(solution)/shard_map/psum | solution.py:56
  267.8 19.8 %copy-start = (f32[2,256,8192]{2,1,0:T(8,128)S(1)}, f32[2,256,8192]{2,1,0:T(8,128)}, u32[]{:S(2)}) copy-start(f32[2,256,8192]{2,1,0:T(8,128)} %all-gather.4.cloned.1.call-done) | copy-start | bytes 50331652
Sparse Core Ops, SparseCore 0:
  9.7 152.3 all-gather.5
  163.7 104.0 all-gather.3
  297.7 23.2 all-reduce.1
where the time goes:
time: 329 us
  waiting for transfers between devices  277 us (84%)
  matrix products  28.9 us (9%)
  between operations  13.2 us (4%)
  local copies, waits for them, and re-layouts  9.38 us (3%)
    all_gather x1, waiting for transfers between devices, local(): right_whole = lax.all_gather(right_own, 'row', axis=1, tiled=True)  148 us
    all_gather x1, waiting for transfers between devices, local(): lax.all_gather(left_own, 'col', axis=2, tiled=True)  106 us
    psum x1, waiting for transfers between devices, local(): product = lax.psum(partial_product, 'layer')  23.4 us
    dot_general x1, matrix products, accumulate(): jnp.dot(left_real, right_real, precision=highest, preferred_element_type=...  9.94 us
    dot_general x1, matrix products, accumulate(): jnp.dot(left_imag, right_imag, precision=highest, preferred_element_type=...  9.81 us
    dot_general x1, matrix products, accumulate(): jnp.dot(left_real + left_imag, right_total, precision=highest, preferred_...  9.2 us
  transfers between devices with their start and end apart: 3, of which 3 were waited for; matrix products, arithmetic and copies ran while one was open for 1% of the time, Pallas kernels for 0%

commit v1 on v0

v1 whole, which is shorter than its diff:
```python
import functools

import jax
import jax.numpy as jnp
from jax import lax
from jax.experimental import pallas as pl
from jax.experimental.pallas import tpu as pltpu
from jax.sharding import PartitionSpec as P

CHUNKS = 8
MESH = pl.DeviceIdType.MESH


def kernel(rows, left, right, out, abuf, bbuf, xbuf, acc, xacc, xout, xin, pout, pin, qout, qin,
           own_sem, bsend, rsend, brecv, ysend, yrecv, xsend, xrecv, csend, crecv, psem, qsem):
    x = lax.axis_index("layer")
    z = lax.axis_index("row")
    col = lax.axis_index("col")
    y = col // 2
    c = col % 2
    height = left.shape[1]
    width = right.shape[2]
    share = abuf.shape[3]
    step = share // CHUNKS
    last = rows - 1
    base = x * share
    parity = z % 2
    at_low, at_high = z == 0, z == last
    at_end = at_low | at_high
    lends = (at_low & (c == 1)) | (at_high & (c == 0))
    helps = ((z == 1) & (c == 1)) | ((z == last - 1) & (c == 0))
    inward = jnp.where(at_low, 1, last - 1)
    outward = jnp.where(z == 1, 0, last)
    lent_slot = jnp.where(at_low, 0, (last - 1) // 2)
    lends_own = lends & (y == lent_slot)
    lends_relayed = lends & (y != lent_slot)

    def other(**where):
        return dict(device_id=where, device_id_type=MESH)

    partner = dict(col=y * 2 + 1 - c)
    across = dict(col=(1 - y) * 2 + c)
    copy_x = dict(layer=1 - x)

    barrier = pltpu.get_barrier_semaphore()
    for where in (partner, across, copy_x):
        pl.semaphore_signal(barrier, inc=1, **other(**where))

    @pl.when(z > 0)
    def _():
        for core in range(2):
            pl.semaphore_signal(barrier, inc=1, **other(row=z - 1, col=y * 2 + core))

    @pl.when(z < last)
    def _():
        for core in range(2):
            pl.semaphore_signal(barrier, inc=1, **other(row=z + 1, col=y * 2 + core))

    own_copy = pltpu.make_async_copy(left.at[:, :, pl.ds(base, share)], abuf.at[y], own_sem)
    own_copy.start()
    acc[...] = jnp.zeros_like(acc)
    xacc[...] = jnp.zeros_like(xacc)
    pl.semaphore_wait(barrier, 3 + 2 * ((z > 0).astype(jnp.int32) + (z < last).astype(jnp.int32)))

    def span(i):
        return pl.ds(pl.multiple_of(i * step, step), step)

    def source_span(i):
        return pl.ds(pl.multiple_of(base + i * step, step), step)

    def half(h):
        return pl.ds(pl.multiple_of(h * width, width), width)

    def b_copy(i, way, row):
        return pltpu.make_async_remote_copy(
            src_ref=right.at[:, source_span(i), :],
            dst_ref=bbuf.at[z // 2, :, span(i), half(c)],
            send_sem=bsend.at[way, i], recv_sem=brecv.at[z // 2, c, i],
            **other(row=row, col=y * 2 + parity))

    def b_local(i):
        return pltpu.make_async_copy(
            right.at[:, source_span(i), :], bbuf.at[z // 2, :, span(i), half(c)],
            brecv.at[z // 2, c, i])

    def y_copy(i):
        return pltpu.make_async_remote_copy(
            src_ref=left.at[:, :, source_span(i)], dst_ref=abuf.at[y, :, :, span(i)],
            send_sem=ysend.at[i], recv_sem=yrecv.at[i], **other(**across))

    def y_arrival(i):
        return pltpu.make_async_remote_copy(
            src_ref=left.at[:, :, source_span(i)], dst_ref=abuf.at[1 - y, :, :, span(i)],
            send_sem=ysend.at[i], recv_sem=yrecv.at[i], **other(**across))

    def x_own(i):
        return pltpu.make_async_remote_copy(
            src_ref=left.at[:, :, source_span(i)], dst_ref=xbuf.at[:, :, span(i)],
            send_sem=xsend.at[i], recv_sem=xrecv.at[i], **other(row=inward))

    def x_relay(i):
        return pltpu.make_async_remote_copy(
            src_ref=abuf.at[1 - y, :, :, span(i)], dst_ref=xbuf.at[:, :, span(i)],
            send_sem=xsend.at[i], recv_sem=xrecv.at[i], **other(row=inward))

    sends_up = (z < last) & (z != last - 1)
    sends_down = (z > 0) & (z != 1)

    def launch(i, carry):
        @pl.when(sends_up)
        def _():
            b_copy(i, 0, z + 1).start()

        @pl.when(sends_down)
        def _():
            b_copy(i, 1, z - 1).start()

        y_copy(i).start()

        @pl.when(c == parity)
        def _():
            b_local(i).start()

        @pl.when(c != parity)
        def _():
            b_copy(i, 2, z).start()

        return carry

    lax.fori_loop(0, CHUNKS, launch, 0)

    @pl.when(lends_own)
    def _():
        def lend(i, carry):
            x_own(i).start()
            return carry
        lax.fori_loop(0, CHUNKS, lend, 0)

    own_copy.wait()

    def b_arrival(s, h, i):
        ref = bbuf.at[s, :, span(i), half(h)]
        return pltpu.make_async_copy(ref, ref, brecv.at[s, h, i])

    def relay(s, h, i, row):
        ref = bbuf.at[s, :, span(i), half(h)]
        return pltpu.make_async_remote_copy(
            src_ref=ref, dst_ref=ref, send_sem=rsend.at[s, h, i], recv_sem=brecv.at[s, h, i],
            **other(row=row))

    def present(s):
        quarter = 2 * s + c
        return jnp.logical_not((at_low & (quarter == 1)) | (at_high & (quarter == last - 1)))

    def goes_up(s):
        quarter = 2 * s + c
        return (quarter < z) & (z < last)

    def goes_down(s):
        quarter = 2 * s + c
        return (quarter > z) & (z > 0)

    def multiply(totals, a_ref, s, i):
        a_re, a_im = a_ref[0, :, span(i)], a_ref[1, :, span(i)]
        b_re, b_im = bbuf[s, 0, span(i), :], bbuf[s, 1, span(i), :]
        dot = functools.partial(
            jnp.dot, precision=lax.Precision.HIGHEST, preferred_element_type=jnp.float32)
        totals[0] += dot(a_re, b_re)
        totals[1] += dot(a_im, b_im)
        totals[2] += dot(a_re + a_im, b_re + b_im)

    def right_step(i):
        for s in range(2):
            @pl.when(present(s))
            def _():
                for h in range(2):
                    b_arrival(s, h, i).wait()

                    @pl.when(goes_up(s))
                    def _():
                        relay(s, h, i, z + 1).start()

                    @pl.when(goes_down(s))
                    def _():
                        relay(s, h, i, z - 1).start()

        @pl.when(present(y))
        def _():
            multiply(acc, abuf.at[y], y, i)

    def left_step(i):
        y_arrival(i).wait_recv()

        @pl.when(lends_relayed)
        def _():
            x_relay(i).start()

        @pl.when(present(1 - y))
        def _():
            multiply(acc, abuf.at[1 - y], 1 - y, i)

        @pl.when(helps)
        def _():
            x_own(i).wait_recv()
            multiply(xacc, xbuf, z // 2, i)

    early = jnp.logical_not(at_end) & (c != parity)

    def work(t, carry):
        first = t < CHUNKS
        apart = jnp.where(first, t, t - CHUNKS)
        i = jnp.where(early | lends_relayed, apart, t // 2)
        is_left = ((early & jnp.logical_not(first)) | (lends_relayed & first)
                   | (jnp.logical_not(early | lends_relayed) & (t % 2 == 1)))

        @pl.when(is_left)
        def _():
            left_step(i)

        @pl.when(jnp.logical_not(is_left))
        def _():
            right_step(i)

        return carry

    lax.fori_loop(0, 2 * CHUNKS, work, 0)

    def combined(totals, h):
        first, second, third = (totals[k, :, half(h)] for k in range(3))
        return first - second, third - first - second

    def lend_back(h):
        return pltpu.make_async_remote_copy(
            src_ref=xout.at[h], dst_ref=xin, send_sem=csend.at[h], recv_sem=crecv,
            **other(row=outward, col=y * 2 + h))

    @pl.when(helps)
    def _():
        for h in range(2):
            xout[h, 0], xout[h, 1] = combined(xacc, h)
        for h in range(2):
            lend_back(h).start()

    pout[0], pout[1] = combined(acc, 1 - c)
    to_partner = pltpu.make_async_remote_copy(
        src_ref=pout, dst_ref=pin, send_sem=psem.at[0], recv_sem=psem.at[1], **other(**partner))
    to_partner.start()
    mine_re, mine_im = combined(acc, c)
    qout[0] = mine_re
    qout[1] = mine_im
    to_partner.wait_recv()
    qout[...] += pin[...]

    @pl.when(at_end)
    def _():
        pltpu.make_async_copy(xin, xin, crecv).wait()
        qout[...] += xin[...]

    to_copy = pltpu.make_async_remote_copy(
        src_ref=qout, dst_ref=qin, send_sem=qsem.at[0], recv_sem=qsem.at[1], **other(**copy_x))
    to_copy.start()

    def settle(i, carry):
        @pl.when(sends_up)
        def _():
            b_copy(i, 0, z).wait_send()

        @pl.when(sends_down)
        def _():
            b_copy(i, 1, z).wait_send()

        @pl.when(c != parity)
        def _():
            b_copy(i, 2, z).wait_send()

        y_copy(i).wait_send()

        @pl.when(lends)
        def _():
            x_own(i).wait_send()

        for s in range(2):
            @pl.when(present(s) & (goes_up(s) | goes_down(s)))
            def _():
                for h in range(2):
                    relay(s, h, i, z).wait_send()

        return carry

    lax.fori_loop(0, CHUNKS, settle, 0)

    @pl.when(helps)
    def _():
        for h in range(2):
            lend_back(h).wait_send()

    to_partner.wait_send()
    to_copy.wait()
    out[...] = qout[...] + qin[...]


def lent_product(left_matrix, right_matrix, layers, rows):
    height = left_matrix.shape[1]
    width = right_matrix.shape[2]
    share = left_matrix.shape[2] // layers
    f32 = jnp.float32
    dma = pltpu.SemaphoreType.DMA
    block = (2, height, width)
    return pl.pallas_call(
        functools.partial(kernel, rows),
        out_shape=jax.ShapeDtypeStruct(block, f32),
        in_specs=[pl.BlockSpec(memory_space=pl.ANY)] * 2,
        out_specs=pl.BlockSpec(memory_space=pltpu.VMEM),
        scratch_shapes=[
            pltpu.VMEM((2, 2, height, share), f32),
            pltpu.VMEM((2, 2, share, 2 * width), f32),
            pltpu.VMEM((2, height, share), f32),
            pltpu.VMEM((3, height, 2 * width), f32),
            pltpu.VMEM((3, height, 2 * width), f32),
            pltpu.VMEM((2,) + block, f32),
            pltpu.VMEM(block, f32),
            pltpu.VMEM(block, f32),
            pltpu.VMEM(block, f32),
            pltpu.VMEM(block, f32),
            pltpu.VMEM(block, f32),
            dma,
            dma((3, CHUNKS)),
            dma((2, 2, CHUNKS)),
            dma((2, 2, CHUNKS)),
            dma((CHUNKS,)),
            dma((CHUNKS,)),
            dma((CHUNKS,)),
            dma((CHUNKS,)),
            dma((2,)),
            dma,
            dma((2,)),
            dma((2,)),
        ],
        compiler_params=pltpu.CompilerParams(
            collective_id=0, has_side_effects=True, vmem_limit_bytes=60 * 2**20),
    )(left_matrix, right_matrix)


def gathered_product(left_matrix, right_matrix, layers):
    layer_index = lax.axis_index("layer")
    local_cols = right_matrix.shape[2]
    left_width = left_matrix.shape[2]
    right_height = right_matrix.shape[1]
    share_width = left_width // layers
    group_count = right_height // left_width
    left_own = lax.dynamic_slice_in_dim(left_matrix, layer_index * share_width, share_width, 2)
    right_view = right_matrix.reshape(2, group_count, layers, share_width, local_cols)
    right_own = lax.dynamic_slice_in_dim(right_view, layer_index, 1, 2)
    right_own = right_own.reshape(2, group_count * share_width, local_cols)
    right_whole = lax.all_gather(right_own, "row", axis=1, tiled=True)
    left_whole = lax.all_gather(left_own, "col", axis=2, tiled=True)
    dot = functools.partial(
        jnp.dot, precision=lax.Precision.HIGHEST, preferred_element_type=jnp.float32)
    first_term = dot(left_whole[0], right_whole[0])
    second_term = dot(left_whole[1], right_whole[1])
    third_term = dot(left_whole[0] + left_whole[1], right_whole[0] + right_whole[1])
    partial_product = jnp.stack([first_term - second_term, third_term - first_term - second_term])
    return lax.psum(partial_product, "layer")


def local(left_matrix, right_matrix):
    layers = lax.axis_size("layer")
    rows = lax.axis_size("row")
    cols = lax.axis_size("col")
    if layers == 2 and rows == cols == 4:
        return lent_product(left_matrix, right_matrix, layers, rows)
    return gathered_product(left_matrix, right_matrix, layers)


def solution(mesh):
    in_specs = (P(None, "row", "col"), P(None, "row", "col"))
    out_specs = P(None, "row", "col")
    return jax.shard_map(local, mesh=mesh, in_specs=in_specs, out_specs=out_specs, check_vma=False)
```

time: 329 us -> 120 us (0.36)
  waiting for transfers between devices: 277 us -> 0 us
  Pallas kernels: 0 us -> 116 us
  matrix products: 28.9 us -> 0 us
  between operations: 13.2 us -> 0.01 us
  local copies, waits for them, and re-layouts: 9.38 us -> 1.67 us
    all_gather x2 -> x0, waiting for transfers between devices: 253 us -> none  [the longest x1 148 us: local(): right_whole = lax.all_gather(right_own, 'row', axis=1, tiled=True)]
    pallas_call x0 -> x1, Pallas kernels: none -> 116 us  [lent_product(): pl.pallas_call(functools.partial(kernel, rows), out_shape=jax.ShapeDtypeS...]
    dot_general x3 -> x0, matrix products: 28.9 us -> none  [the longest x1 9.94 us: accumulate(): jnp.dot(left_real, right_real, precision=highest, preferred_element_type=...]
    psum x1 -> x0, waiting for transfers between devices: 23.4 us -> none  [local(): product = lax.psum(partial_product, 'layer')]
    dynamic_slice x2 -> x0, local copies, waits for them, and re-layouts: 7.71 us -> none  [the longest x1 4.65 us: local(): lax.dynamic_slice_in_dim(left_matrix, layer_index * share_width, share_wi...]
  transfers between devices with their start and end apart: 3 -> 0, of which waited for: 3 -> 0; matrix products, arithmetic and copies ran while one was open for 1% -> 0% of each run, Pallas kernels for 0% -> 0%
where the time goes in v1:
time: 120 us; the launch traced here: 118 us
  Pallas kernels  116 us (97%)
  local copies, waits for them, and re-layouts  1.67 us (1%)
    pallas_call x1, Pallas kernels, lent_product(): pl.pallas_call(functools.partial(kernel, rows), out_shape=jax.ShapeDtypeS...  116 us

profile of v1, /device:TPU:0, one launch (start us, length us, event | category | flops | bytes accessed | tf_op | source)
XLA Modules:
  0.0 117.8 jit_solution(17340034999339530929)
XLA Ops:
  0.0 116.1 %shard_map.28 = f32[2,256,128]{2,1,0:T(8,128)} custom-call(f32[2,256,4096]{2,1,0:T(8,128)} %left.1, f32[2,4096,128]{2,1,0:T(8,128)} %right.1), custom_call_target="tpu_custom_call" | custom-call | tf_op jit(solution)/shard_map/pallas_call | solution.py:309
  116.1 1.7 %copy.4 = f32[2,256,128]{2,1,0:T(8,128)} copy(f32[2,256,128]{2,1,0:T(8,128)} %shard_map.28) | data formatting | bytes 524288

commit v2 on v1

--- a/solution.py
+++ b/solution.py
@@ -7,12 +7,12 @@
 from jax.experimental.pallas import tpu as pltpu
 from jax.sharding import PartitionSpec as P
 
-CHUNKS = 8
+CHUNKS = 16
 MESH = pl.DeviceIdType.MESH
 
 
 def kernel(rows, left, right, out, abuf, bbuf, xbuf, acc, xacc, xout, xin, pout, pin, qout, qin,
-           own_sem, bsend, rsend, brecv, ysend, yrecv, xsend, xrecv, csend, crecv, psem, qsem):
+           own_sem, bsend, rsend, brecv, ysend, yrecv, xsend, xrecv, csend, crecv, psem, qsem, turn):
     x = lax.axis_index("layer")
     z = lax.axis_index("row")
     col = lax.axis_index("col")
@@ -74,13 +74,13 @@
     def b_copy(i, way, row):
         return pltpu.make_async_remote_copy(
             src_ref=right.at[:, source_span(i), :],
-            dst_ref=bbuf.at[z // 2, :, span(i), half(c)],
+            dst_ref=bbuf.at[z // 2, c, :, span(i), :],
             send_sem=bsend.at[way, i], recv_sem=brecv.at[z // 2, c, i],
             **other(row=row, col=y * 2 + parity))
 
     def b_local(i):
         return pltpu.make_async_copy(
-            right.at[:, source_span(i), :], bbuf.at[z // 2, :, span(i), half(c)],
+            right.at[:, source_span(i), :], bbuf.at[z // 2, c, :, span(i), :],
             brecv.at[z // 2, c, i])
 
     def y_copy(i):
@@ -103,6 +103,7 @@
             src_ref=abuf.at[1 - y, :, :, span(i)], dst_ref=xbuf.at[:, :, span(i)],
             send_sem=xsend.at[i], recv_sem=xrecv.at[i], **other(row=inward))
 
+    yields = at_end & jnp.logical_not(lends) & (y == lent_slot)
     sends_up = (z < last) & (z != last - 1)
     sends_down = (z > 0) & (z != 1)
 
@@ -115,7 +116,9 @@
         def _():
             b_copy(i, 1, z - 1).start()
 
-        y_copy(i).start()
+        @pl.when(jnp.logical_not(yields))
+        def _():
+            y_copy(i).start()
 
         @pl.when(c == parity)
         def _():
@@ -136,14 +139,31 @@
             return carry
         lax.fori_loop(0, CHUNKS, lend, 0)
 
+    @pl.when(lends_own)
+    def _():
+        def crossed(i, carry):
+            y_copy(i).wait_send()
+            return carry
+        lax.fori_loop(0, CHUNKS - 1, crossed, 0)
+        pl.semaphore_signal(turn, inc=1, **other(**partner))
+
+    @pl.when(yields)
+    def _():
+        pl.semaphore_wait(turn, 1)
+
+        def cross(i, carry):
+            y_copy(i).start()
+            return carry
+        lax.fori_loop(0, CHUNKS, cross, 0)
+
     own_copy.wait()
 
     def b_arrival(s, h, i):
-        ref = bbuf.at[s, :, span(i), half(h)]
+        ref = bbuf.at[s, h, :, span(i), :]
         return pltpu.make_async_copy(ref, ref, brecv.at[s, h, i])
 
     def relay(s, h, i, row):
-        ref = bbuf.at[s, :, span(i), half(h)]
+        ref = bbuf.at[s, h, :, span(i), :]
         return pltpu.make_async_remote_copy(
             src_ref=ref, dst_ref=ref, send_sem=rsend.at[s, h, i], recv_sem=brecv.at[s, h, i],
             **other(row=row))
@@ -160,14 +180,29 @@
         quarter = 2 * s + c
         return (quarter > z) & (z > 0)
 
+    def split(value):
+        high = value.astype(jnp.bfloat16)
+        return high, (value - high.astype(jnp.float32)).astype(jnp.bfloat16)
+
+    def dot(a, b):
+        a_high, a_low = split(a)
+        b_high, b_low = split(b)
+        return jnp.dot(
+            jnp.concatenate([a_high, a_high, a_low], axis=1),
+            jnp.concatenate([b_high, b_low, b_high], axis=0),
+            preferred_element_type=jnp.float32)
+
     def multiply(totals, a_ref, s, i):
-        a_re, a_im = a_ref[0, :, span(i)], a_ref[1, :, span(i)]
-        b_re, b_im = bbuf[s, 0, span(i), :], bbuf[s, 1, span(i), :]
-        dot = functools.partial(
-            jnp.dot, precision=lax.Precision.HIGHEST, preferred_element_type=jnp.float32)
-        totals[0] += dot(a_re, b_re)
-        totals[1] += dot(a_im, b_im)
-        totals[2] += dot(a_re + a_im, b_re + b_im)
+        @pl.when(i % 2 == 1)
+        def _():
+            at = pl.ds(pl.multiple_of((i - 1) * step, 2 * step), 2 * step)
+            a_re, a_im = a_ref[0, :, at], a_ref[1, :, at]
+            b_re, b_im = (
+                jnp.concatenate([bbuf[s, h, k, at, :] for h in range(2)], axis=1)
+                for k in range(2))
+            totals[0] += dot(a_re, b_re)
+            totals[1] += dot(a_im, b_im)
+            totals[2] += dot(a_re + a_im, b_re + b_im)
 
     def right_step(i):
         for s in range(2):
@@ -273,7 +308,9 @@
         def _():
             b_copy(i, 2, z).wait_send()
 
-        y_copy(i).wait_send()
+        @pl.when(jnp.logical_not(lends_own & (i < CHUNKS - 1)))
+        def _():
+            y_copy(i).wait_send()
 
         @pl.when(lends)
         def _():
@@ -313,7 +350,7 @@
         out_specs=pl.BlockSpec(memory_space=pltpu.VMEM),
         scratch_shapes=[
             pltpu.VMEM((2, 2, height, share), f32),
-            pltpu.VMEM((2, 2, share, 2 * width), f32),
+            pltpu.VMEM((2, 2, 2, share, width), f32),
             pltpu.VMEM((2, height, share), f32),
             pltpu.VMEM((3, height, 2 * width), f32),
             pltpu.VMEM((3, height, 2 * width), f32),
@@ -335,6 +372,7 @@
             dma,
             dma((2,)),
             dma((2,)),
+            pltpu.SemaphoreType.REGULAR,
         ],
         compiler_params=pltpu.CompilerParams(
             collective_id=0, has_side_effects=True, vmem_limit_bytes=60 * 2**20),

time: 120 us -> 118 us (0.983)
  Pallas kernels: 116 us -> 114 us
    pallas_call x1, Pallas kernels: 116 us -> 114 us  [lent_product(): pl.pallas_call(functools.partial(kernel, rows), out_shape=jax.ShapeDtypeS...]
where the time goes in v2:
time: 118 us; the launch traced here: 116 us
  Pallas kernels  114 us (97%)
  local copies, waits for them, and re-layouts  1.67 us (1%)
    pallas_call x1, Pallas kernels, lent_product(): pl.pallas_call(functools.partial(kernel, rows), out_shape=jax.ShapeDtypeS...  114 us

profile of v2, /device:TPU:0, one launch (start us, length us, event | category | flops | bytes accessed | tf_op | source)
XLA Modules:
  0.0 116.1 jit_solution(9828717473592760929)
XLA Ops:
  0.0 114.4 %shard_map.28 = f32[2,256,128]{2,1,0:T(8,128)} custom-call(f32[2,256,4096]{2,1,0:T(8,128)} %left.1, f32[2,4096,128]{2,1,0:T(8,128)} %right.1), custom_call_target="tpu_custom_call" | custom-call | tf_op jit(solution)/shard_map/pallas_call | solution.py:346
  114.4 1.7 %copy.4 = f32[2,256,128]{2,1,0:T(8,128)} copy(f32[2,256,128]{2,1,0:T(8,128)} %shard_map.28) | data formatting | bytes 524288
